TPU v7x, 512 devices: a whole 4x8x8 slice. The times are simulated.
512 devices in a mesh: band: 16 (over y, z_lo), ga: 32 (over x, z_hi, core).
Axes of the slice: x: 4, y: 8, z: 8 (z_hi: 4, z_lo: 2; z = z_hi * 2 + z_lo), core: 2. Of those that a mesh axis runs over, the one named last changes fastest.
Arguments:
- orbitals: bfloat16 [32768, 4096], P('ga', 'band'), may hold values from -6 to 6
Outputs:
- margin: float32 [4096, 4096], P('band', 'ga')
- corrected: bfloat16 [32768, 4096], P('ga', 'band')
All inputs are finite; a program needn't handle non-finite values.
Results may differ from a plain program's by a relative error of at most 0.0056.
Values may be sent and summed in bfloat16 or wider, within the bound.
A program may use at most 64 MiB of HBM per device.

v0:
```python
import jax
import jax.numpy as jnp
from jax import lax
from jax.sharding import Mesh
from jax.sharding import PartitionSpec as P

BAND = ("band_0", "band_1")


def whole_of(value, axes, dim):
    if not axes:
        return value
    nearer = lax.all_gather(value, axes[-1], axis=dim, tiled=True)
    return whole_of(nearer, axes[:-1], dim)


def split_up(value, dim, count):
    before, after = (value.shape[:dim], value.shape[dim + 1 :])
    return jnp.moveaxis(value.reshape(*before, count, -1, *after), dim, 0)


def sum_at_owner(value, axis, dim):
    blocks = split_up(value, dim, lax.axis_size(axis))
    arrived = lax.all_to_all(blocks, axis, split_axis=0, concat_axis=0, tiled=True)
    return arrived.astype(jnp.float32).sum(axis=0)


def in_order(blocks, dim):
    dims = list(blocks.shape[1:])
    dims[dim] *= blocks.shape[0]
    return jnp.moveaxis(blocks, 0, dim).reshape(dims)


def sent_to_all(value, axis):
    count = lax.axis_size(axis)
    return lax.all_to_all(
        jnp.broadcast_to(value[None], (count, *value.shape)), axis, 0, 0, tiled=True
    )


def gathered_copies(value, axis, dim):
    return in_order(sent_to_all(value, axis), dim)


def identity_block(rows, cols, row_start, col_start):
    row_index = row_start + lax.iota(jnp.int32, rows)
    col_index = col_start + lax.iota(jnp.int32, cols)
    return (row_index[:, None] == col_index[None, :]).astype(jnp.float32)


def shards(orbitals):
    own_coeffs = orbitals.shape[0]
    own_bands = orbitals.shape[1]
    all_bands = own_bands * lax.axis_size(BAND)
    all_coeffs = own_coeffs * lax.axis_size("ga")
    col_width = all_bands // lax.axis_size("ga")
    row_start = lax.axis_index(BAND) * own_bands
    col_start = lax.axis_index("ga") * col_width
    everyone = whole_of(orbitals, BAND, 1)
    partial_value = lax.dot_general(
        orbitals, everyone, (((0,), (0,)), ((), ())), preferred_element_type=jnp.float32
    )
    unit_block = identity_block(own_bands, col_width, row_start, col_start)
    margin_block = sum_at_owner(partial_value.astype(jnp.bfloat16), "ga", 1) / all_coeffs
    deviation_block = margin_block - unit_block
    deviation_rows = lax.all_gather(
        deviation_block.astype(jnp.bfloat16), "ga", axis=1, tiled=True
    ).astype(deviation_block.dtype)
    deviation_cols = gathered_copies(deviation_block.astype(jnp.bfloat16), BAND, 0).astype(
        deviation_block.dtype
    )
    square = jnp.dot(
        deviation_rows,
        deviation_cols,
        precision=lax.Precision.HIGHEST,
        preferred_element_type=jnp.float32,
    )
    fix_block = (unit_block - 0.5 * deviation_block + 0.375 * square).astype(jnp.bfloat16)
    fix_rows = gathered_copies(fix_block, "ga", 1)
    corrected = lax.dot_general(
        everyone, fix_rows, (((1,), (1,)), ((), ())), preferred_element_type=jnp.float32
    )
    return (margin_block, corrected.astype(jnp.bfloat16))


def solution(mesh):
    finer = Mesh(mesh.devices.reshape(8, 2, mesh.shape["ga"]), ("band_0", "band_1", "ga"))
    placed = (P("ga", BAND),)
    return jax.shard_map(
        shards,
        mesh=finer,
        in_specs=placed,
        out_specs=(P(BAND, "ga"), P("ga", BAND)),
        check_vma=False,
    )
```

profile of v0, /device:TPU:1, one launch (start us, length us, event | category | flops | bytes accessed | tf_op | source)
XLA Modules:
  0.0 347.4 jit_solution(5040010379792881687)
XLA Ops:
  7.2 0.0 all-gather.4.cloned.1.call-start
  7.2 0.7 all-gather.4.cloned.1.call-update
  7.9 0.0 all-gather.6.cloned.1.call-start
  7.9 36.7 %all-gather.4.cloned.1.call-done = bf16[1024,512]{1,0:T(8,128)(2,1)} async-done(((bf16[1024,256]{1,0:T(8,128)(2,1)}), bf16[1024,512]{1,0:T(8,128)(2,1)}) %all-gather.4.cloned.1.call-update) | async-done | bytes 1048592 | tf_op jit(solution)/shard_map/all_gather | solution.py:13
  44.7 0.0 all-gather.6.cloned.1.call-update
  44.7 98.9 %all-gather.6.cloned.1.call-done = bf16[1024,4096]{1,0:T(8,128)(2,1)} async-done(((bf16[1024,512]{1,0:T(8,128)(2,1)}), bf16[1024,4096]{1,0:T(8,128)(2,1)}) %all-gather.6.cloned.1.call-update) | async-done | bytes 8388624 | tf_op jit(solution)/shard_map/all_gather | solution.py:13
  143.6 6.0 %fusion = bf16[32,32,8,128]{3,2,1,0:T(8,128)(2,1)S(1)} fusion(bf16[1024,256]{1,0:T(8,128)(2,1)} %param.1, bf16[1024,4096]{1,0:T(8,128)(2,1)} %all-gather.6.cloned.1.call-done), kind=kOutput, calls=%fused_computation.3 | convolution fusion | flops 2148532224 | bytes 11010048 | tf_op jit(solution)/shard_map/dot_general | solution.py:60
  149.6 1.9 copy.11
  151.5 10.8 %all-to-all-start = ((bf16[32,256,128]{2,1,0:T(8,128)(2,1)}), bf16[32,256,128]{2,1,0:T(8,128)(2,1)S(1)}, u32[]{:S(2)}, u32[]{:S(2)}) async-start(bf16[32,256,128]{2,1,0:T(8,128)(2,1)} %bitcast.20), calls=%async_computation | async-start | bytes 4194304 | tf_op jit(solution)/shard_map/all_to_all | solution.py:24
  162.3 0.0 all-gather.8.cloned.1.call-start
  162.4 51.7 %all-to-all-done = bf16[32,256,128]{2,1,0:T(8,128)(2,1)S(1)} async-done(((bf16[32,256,128]{2,1,0:T(8,128)(2,1)}), bf16[32,256,128]{2,1,0:T(8,128)(2,1)S(1)}, u32[]{:S(2)}, u32[]{:S(2)}) %all-to-all-start) | async-done | bytes 2097184 | tf_op jit(solution)/shard_map/all_to_all | solution.py:24
  214.0 0.3 convert_reduce_fusion
  214.3 0.7 fusion.4
  215.1 0.0 all-gather.8.cloned.1.call-update
  215.1 1.1 broadcast_in_dim.4
  216.2 30.9 %all_to_all.15 = bf16[16,256,128]{2,1,0:T(8,128)(2,1)S(1)} all-to-all(bf16[16,256,128]{2,1,0:T(8,128)(2,1)S(1)} %broadcast_in_dim.4), channel_id=1, replica_groups=mesh['band_0'=8,'band_1'=2,'ga'=32] {'band_0','band_1'}, dimensions={0} | all-to-all | bytes 2097152 | tf_op jit(solution)/shard_map/all_to_all | solution.py:36
  247.1 27.0 %all-gather.8.cloned.1.call-done = bf16[256,4096]{1,0:T(8,128)(2,1)} async-done(((bf16[256,128]{1,0:T(8,128)(2,1)}), bf16[256,4096]{1,0:T(8,128)(2,1)}) %all-gather.8.cloned.1.call-update) | async-done | bytes 2097168 | tf_op jit(solution)/shard_map/all_gather | solution.py:66
  274.1 2.3 fusion.3
  276.4 0.0 copy-done
  276.4 0.1 copy.7
  276.5 0.2 broadcast_in_dim.5
  276.8 57.4 %all_to_all.16 = bf16[32,256,128]{1,2,0:T(8,128)(2,1)S(1)} all-to-all(bf16[32,256,128]{1,2,0:T(8,128)(2,1)S(1)} %broadcast_in_dim.5), channel_id=1, replica_groups=mesh['band_0'=8,'band_1'=2,'ga'=32] {'ga'}, dimensions={0} | all-to-all | bytes 4194304 | tf_op jit(solution)/shard_map/all_to_all | solution.py:36
  334.1 5.8 %fusion.1 = bf16[1024,256]{0,1:T(8,128)(2,1)S(1)} fusion(bf16[256,4096]{0,1:T(8,128)(2,1)S(1)} %bitcast.22, bf16[1024,4096]{1,0:T(8,128)(2,1)} %all-gather.6.cloned.1.call-done), kind=kOutput, calls=%fused_computation.5 | convolution fusion | flops 2147745792 | bytes 11010048 | tf_op jit(solution)/shard_map/dot_general | solution.py:80
  339.9 1.0 copy.8
  (3 shorter events, 0.0 us)
Async XLA Ops:
  7.2 37.5 %all-gather.4.cloned.1.call-start = ((), (), s32[]{:S(2)}) async-start(), calls=%async_computation.3 | async-start | bytes 1572864 | tf_op jit(solution)/shard_map/all_gather | solution.py:13
  7.9 135.7 %all-gather.6.cloned.1.call-start = ((), (), s32[]{:S(2)}) async-start(), calls=%async_computation.4 | async-start | bytes 9437184 | tf_op jit(solution)/shard_map/all_gather | solution.py:13
  151.5 62.5 %all-to-all-start = ((bf16[32,256,128]{2,1,0:T(8,128)(2,1)}), bf16[32,256,128]{2,1,0:T(8,128)(2,1)S(1)}, u32[]{:S(2)}, u32[]{:S(2)}) async-start(bf16[32,256,128]{2,1,0:T(8,128)(2,1)} %bitcast.20), calls=%async_computation | async-start | bytes 4194304 | tf_op jit(solution)/shard_map/all_to_all | solution.py:24
  162.3 111.8 %all-gather.8.cloned.1.call-start = ((), (), s32[]{:S(2)}) async-start(), calls=%async_computation.5 | async-start | bytes 2162688 | tf_op jit(solution)/shard_map/all_gather | solution.py:66
  215.1 61.4 %copy-start = (f32[256,128]{1,0:T(8,128)}, f32[256,128]{1,0:T(8,128)S(1)}, u32[]{:S(2)}) copy-start(f32[256,128]{1,0:T(8,128)S(1)} %get-tuple-element.9) | copy-start | bytes 393220
Sparse Core Ops, SparseCore 0:
  10.0 34.5 all-gather.3
  46.8 96.7 all-gather.5
  215.2 58.8 all-gather.7
where the time goes:
time: 348 us; the launch traced here: 347 us
  waiting for transfers between devices  215 us (62%)
  blocking collectives  88.3 us (25%)
  matrix products  14 us (4%)
  between operations  13.8 us (4%)
  starting transfers between devices  10.9 us (3%)
  local copies, waits for them, and re-layouts  4.35 us (1%)
    all_gather x2, waiting for transfers between devices, whole_of(): nearer = lax.all_gather(value, axes[-1], axis=dim, tiled=True)  136 us
    all_to_all x2, blocking collectives, sent_to_all(): lax.all_to_all(jnp.broadcast_to(value[None], (count, *value.shape)), axis...  88.3 us
    all_to_all x1, waiting for transfers between devices, sum_at_owner(): lax.all_to_all(blocks, axis, split_axis=0, concat_axis=0, tiled=True)  51.7 us
    all_gather x1, waiting for transfers between devices, shards(): lax.all_gather(deviation_block.astype(jnp.bfloat16), 'ga', axis=1, tiled=...  27 us
    all_to_all x1, starting transfers between devices, sum_at_owner(): lax.all_to_all(blocks, axis, split_axis=0, concat_axis=0, tiled=True)  10.8 us
  transfers between devices with their start and end apart: 4, of which 4 were waited for; matrix products, arithmetic and copies ran while one was open for 0% of the time, Pallas kernels for 0%

commit v1 on v0

--- a/solution.py
+++ b/solution.py
@@ -5,6 +5,11 @@
 from jax.sharding import PartitionSpec as P
 
 BAND = ("band_0", "band_1")
+
+
+def gather_over(array, axis, dim):
+    stack = jnp.stack([array] * lax.axis_size(axis))
+    return jnp.concatenate(lax.all_to_all(stack, axis, 0, 0), axis=dim)
 
 
 def whole_of(value, axes, dim):
@@ -63,9 +68,9 @@
     unit_block = identity_block(own_bands, col_width, row_start, col_start)
     margin_block = sum_at_owner(partial_value.astype(jnp.bfloat16), "ga", 1) / all_coeffs
     deviation_block = margin_block - unit_block
-    deviation_rows = lax.all_gather(
-        deviation_block.astype(jnp.bfloat16), "ga", axis=1, tiled=True
-    ).astype(deviation_block.dtype)
+    deviation_rows = gather_over(deviation_block.astype(jnp.bfloat16), "ga", 1).astype(
+        deviation_block.dtype
+    )
     deviation_cols = gathered_copies(deviation_block.astype(jnp.bfloat16), BAND, 0).astype(
         deviation_block.dtype
     )

time: 348 us -> 377 us (1.083)
  blocking collectives: 88.3 us -> 117 us
  starting transfers between devices: 10.9 us -> 15.2 us
    all_to_all x0 -> x1, blocking collectives: none -> 59.9 us  [gather_over(): return jnp.concatenate(lax.all_to_all(stack, axis, 0, 0), axis=dim)]
    all_to_all x2 -> x1, blocking collectives: 88.3 us -> 57.1 us  [sent_to_all(): lax.all_to_all(jnp.broadcast_to(value[None], (count, *value.shape)), axis...]
    all_gather x1 -> x0, waiting for transfers between devices: 27 us -> none  [shards(): lax.all_gather(deviation_block.astype(jnp.bfloat16), 'ga', axis=1, tiled=...]
    all_to_all x0 -> x1, waiting for transfers between devices: none -> 24.6 us  [sent_to_all(): lax.all_to_all(jnp.broadcast_to(value[None], (count, *value.shape)), axis...]
    all_to_all x0 -> x1, starting transfers between devices: none -> 4.29 us  [sent_to_all(): lax.all_to_all(jnp.broadcast_to(value[None], (count, *value.shape)), axis...]
where the time goes in v1:
time: 377 us
  waiting for transfers between devices  213 us (56%)
  blocking collectives  117 us (31%)
  starting transfers between devices  15.2 us (4%)
  between operations  14.1 us (4%)
  matrix products  12.5 us (3%)
  local copies, waits for them, and re-layouts  4.88 us (1%)
    all_gather x2, waiting for transfers between devices, whole_of(): nearer = lax.all_gather(value, axes[-1], axis=dim, tiled=True)  136 us
    all_to_all x1, blocking collectives, gather_over(): return jnp.concatenate(lax.all_to_all(stack, axis, 0, 0), axis=dim)  59.9 us
    all_to_all x1, blocking collectives, sent_to_all(): lax.all_to_all(jnp.broadcast_to(value[None], (count, *value.shape)), axis...  57.1 us
    all_to_all x1, waiting for transfers between devices, sum_at_owner(): lax.all_to_all(blocks, axis, split_axis=0, concat_axis=0, tiled=True)  51.7 us
    all_to_all x1, waiting for transfers between devices, sent_to_all(): lax.all_to_all(jnp.broadcast_to(value[None], (count, *value.shape)), axis...  24.6 us
    all_to_all x1, starting transfers between devices, sum_at_owner(): lax.all_to_all(blocks, axis, split_axis=0, concat_axis=0, tiled=True)  10.8 us
  transfers between devices with their start and end apart: 4, of which 4 were waited for; matrix products, arithmetic and copies ran while one was open for 0% of the time, Pallas kernels for 0%

profile of v1, /device:TPU:1, one launch (start us, length us, event | category | flops | bytes accessed | tf_op | source)
XLA Modules:
  0.0 376.7 jit_solution(6160965195413190843)
XLA Ops:
  7.2 0.0 all-gather.3.cloned.1.call-start
  7.2 0.7 all-gather.3.cloned.1.call-update
  7.9 0.0 all-gather.5.cloned.1.call-start
  7.9 36.7 %all-gather.3.cloned.1.call-done = bf16[1024,512]{1,0:T(8,128)(2,1)} async-done(((bf16[1024,256]{1,0:T(8,128)(2,1)}), bf16[1024,512]{1,0:T(8,128)(2,1)}) %all-gather.3.cloned.1.call-update) | async-done | bytes 1048592 | tf_op jit(solution)/shard_map/all_gather | solution.py:18
  44.7 0.0 all-gather.5.cloned.1.call-update
  44.7 98.9 %all-gather.5.cloned.1.call-done = bf16[1024,4096]{1,0:T(8,128)(2,1)} async-done(((bf16[1024,512]{1,0:T(8,128)(2,1)}), bf16[1024,4096]{1,0:T(8,128)(2,1)}) %all-gather.5.cloned.1.call-update) | async-done | bytes 8388624 | tf_op jit(solution)/shard_map/all_gather | solution.py:18
  143.6 6.0 %fusion = bf16[32,32,8,128]{3,2,1,0:T(8,128)(2,1)S(1)} fusion(bf16[1024,256]{1,0:T(8,128)(2,1)} %param.1, bf16[1024,4096]{1,0:T(8,128)(2,1)} %all-gather.5.cloned.1.call-done), kind=kOutput, calls=%fused_computation.3 | convolution fusion | flops 2148532224 | bytes 11010048 | tf_op jit(solution)/shard_map/dot_general | solution.py:65
  149.6 1.9 copy.13
  151.5 10.8 %all-to-all-start = ((bf16[32,256,128]{2,1,0:T(8,128)(2,1)}), bf16[32,256,128]{2,1,0:T(8,128)(2,1)S(1)}, u32[]{:S(2)}, u32[]{:S(2)}) async-start(bf16[32,256,128]{2,1,0:T(8,128)(2,1)} %bitcast.23), calls=%async_computation | async-start | bytes 4194304 | tf_op jit(solution)/shard_map/all_to_all | solution.py:29
  162.3 51.7 %all-to-all-done = bf16[32,256,128]{2,1,0:T(8,128)(2,1)S(1)} async-done(((bf16[32,256,128]{2,1,0:T(8,128)(2,1)}), bf16[32,256,128]{2,1,0:T(8,128)(2,1)S(1)}, u32[]{:S(2)}, u32[]{:S(2)}) %all-to-all-start) | async-done | bytes 2097184 | tf_op jit(solution)/shard_map/all_to_all | solution.py:29
  214.0 0.3 convert_reduce_fusion
  214.3 0.1 fusion.4
  214.5 1.3 broadcast_in_dim.4
  215.7 4.3 %all-to-all-start.2 = ((bf16[16,256,128]{2,1,0:T(8,128)(2,1)}), bf16[16,256,128]{2,1,0:T(8,128)(2,1)S(1)}, u32[]{:S(2)}, u32[]{:S(2)}) async-start(bf16[16,256,128]{2,1,0:T(8,128)(2,1)} %broadcast_in_dim.4), calls=%async_computation.2 | async-start | bytes 2097152 | tf_op jit(solution)/shard_map/all_to_all | solution.py:41
  220.0 0.1 copy.8
  220.1 24.6 %all-to-all-done.2 = bf16[16,256,128]{2,1,0:T(8,128)(2,1)S(1)} async-done(((bf16[16,256,128]{2,1,0:T(8,128)(2,1)}), bf16[16,256,128]{2,1,0:T(8,128)(2,1)S(1)}, u32[]{:S(2)}, u32[]{:S(2)}) %all-to-all-start.2) | async-done | bytes 1048608 | tf_op jit(solution)/shard_map/all_to_all | solution.py:41
  244.8 0.2 stack.2
  245.0 59.9 %all_to_all.20 = bf16[32,256,128]{1,2,0:T(8,128)(2,1)S(1)} all-to-all(bf16[32,256,128]{1,2,0:T(8,128)(2,1)S(1)} %stack.2), channel_id=1, replica_groups=mesh['band_0'=8,'band_1'=2,'ga'=32] {'ga'}, dimensions={0} | all-to-all | bytes 4194304 | tf_op jit(solution)/shard_map/all_to_all | solution.py:12
  304.9 0.8 fusion.3
  305.6 0.1 copy.9
  305.7 0.2 broadcast_in_dim.5
  306.0 57.1 %all_to_all.21 = bf16[32,256,128]{1,2,0:T(8,128)(2,1)S(1)} all-to-all(bf16[32,256,128]{1,2,0:T(8,128)(2,1)S(1)} %broadcast_in_dim.5), channel_id=1, replica_groups=mesh['band_0'=8,'band_1'=2,'ga'=32] {'ga'}, dimensions={0} | all-to-all | bytes 4194304 | tf_op jit(solution)/shard_map/all_to_all | solution.py:41
  363.1 5.8 %fusion.1 = bf16[1024,256]{0,1:T(8,128)(2,1)S(1)} fusion(bf16[256,4096]{0,1:T(8,128)(2,1)S(1)} %bitcast.26, bf16[1024,4096]{1,0:T(8,128)(2,1)} %all-gather.5.cloned.1.call-done), kind=kOutput, calls=%fused_computation.5 | convolution fusion | flops 2147745792 | bytes 11010048 | tf_op jit(solution)/shard_map/dot_general | solution.py:85
  368.8 1.0 copy.10
  (4 shorter events, 0.0 us)
Async XLA Ops:
  7.2 37.5 %all-gather.3.cloned.1.call-start = ((), (), s32[]{:S(2)}) async-start(), calls=%async_computation.4 | async-start | bytes 1572864 | tf_op jit(solution)/shard_map/all_gather | solution.py:18
  7.9 135.7 %all-gather.5.cloned.1.call-start = ((), (), s32[]{:S(2)}) async-start(), calls=%async_computation.5 | async-start | bytes 9437184 | tf_op jit(solution)/shard_map/all_gather | solution.py:18
  151.5 62.5 %all-to-all-start = ((bf16[32,256,128]{2,1,0:T(8,128)(2,1)}), bf16[32,256,128]{2,1,0:T(8,128)(2,1)S(1)}, u32[]{:S(2)}, u32[]{:S(2)}) async-start(bf16[32,256,128]{2,1,0:T(8,128)(2,1)} %bitcast.23), calls=%async_computation | async-start | bytes 4194304 | tf_op jit(solution)/shard_map/all_to_all | solution.py:29
  214.4 90.4 %copy-start = (f32[256,128]{1,0:T(8,128)}, f32[256,128]{1,0:T(8,128)S(1)}, u32[]{:S(2)}) copy-start(f32[256,128]{1,0:T(8,128)S(1)} %get-tuple-element.9) | copy-start | bytes 393220
  215.7 29.0 %all-to-all-start.2 = ((bf16[16,256,128]{2,1,0:T(8,128)(2,1)}), bf16[16,256,128]{2,1,0:T(8,128)(2,1)S(1)}, u32[]{:S(2)}, u32[]{:S(2)}) async-start(bf16[16,256,128]{2,1,0:T(8,128)(2,1)} %broadcast_in_dim.4), calls=%async_computation.2 | async-start | bytes 2097152 | tf_op jit(solution)/shard_map/all_to_all | solution.py:41
Sparse Core Ops, SparseCore 0:
  10.0 34.5 all-gather.2
  46.8 96.7 all-gather.4
